TPU v7x, 32 devices: a whole 2x2x4 slice. The times are simulated.
32 devices in a mesh: bank: 4 (over x, core), lane: 8 (over z, y).
Axes of the slice: x: 2, y: 2, z: 4, core: 2. Of those that a mesh axis runs over, the one named last changes fastest.
Arguments:
- amplitudes: float32 [2, 256, 128, 128], P(None, ('bank', 'lane')), may hold values from -6 to 6
- energies: float32 [256, 128, 128], P(('bank', 'lane')), may hold values from -2 to 2
- diagonal_angles: float32 [2, 128], replicated, may hold values from 0.3 to 1.2
Outputs:
- final_parts: float32 [2, 256, 128, 128], P(None, ('bank', 'lane'))
- marginal: float32 [64, 128, 128], P('lane', 'bank')
All inputs are finite; a program needn't handle non-finite values.
Results may differ from a plain program's by a relative error of at most 0.0003.
Values sent between devices are 32-bit elements; how exact they have to be, the bound alone decides.
A program may use at most 64 MiB of HBM per device.

v0:
```python
import functools

import jax
import jax.numpy as jnp
import numpy as np
from jax import lax
from jax.experimental import pallas as pl
from jax.experimental.pallas import tpu as pltpu
from jax.sharding import PartitionSpec as P

MESH = pl.DeviceIdType.MESH
TABLE = 256
SUB = 8


def walsh_table():
    rank = np.arange(TABLE)
    both = rank[:, None] & rank[None, :]
    parity = sum((both >> place) & 1 for place in range(8)) % 2
    return jnp.asarray(np.where(parity == 1, -1.0, 1.0) / 16.0, jnp.bfloat16)


def cos_sin(turn):
    half = turn * 0.5
    x = half * half
    s = -1.0 / 39916800.0
    for term in (1.0 / 362880.0, -1.0 / 5040.0, 1.0 / 120.0, -1.0 / 6.0, 1.0):
        s = s * x + term
    s = s * half
    c = 1.0 / 479001600.0
    for term in (-1.0 / 3628800.0, 1.0 / 40320.0, -1.0 / 720.0, 1.0 / 24.0, -0.5, 1.0):
        c = c * x + term
    return 1.0 - 2.0 * (s * s), 2.0 * (s * c)


def split(values):
    high = values.astype(jnp.bfloat16)
    return high, (values - high.astype(jnp.float32)).astype(jnp.bfloat16)


def mix(items):
    items, step = list(items), 1
    while step < len(items):
        for low in range(len(items)):
            if not low & step:
                u, v = items[low], items[low + step]
                items[low], items[low + step] = u + v, u - v
        step *= 2
    return items


def dot(a, b):
    return jnp.dot(a, b, preferred_element_type=jnp.float32)


def mix_lanes(values, table):
    high, low = split(values)
    return dot(jnp.concatenate([high, low], axis=1), table[:, :128])


def kernel(
    n_bank, n_lane, chunks,
    a_hbm, e_hbm, angle_hbm, table_hbm,
    out_ref, marginal_ref,
    a_ref, e_ref, angle_ref, table_ref,
    held, sent1, got1, sent2, got2, levels, cosine, sine, chance, chances,
    in_sem, e_send, e_recv, send1, recv1, send2, recv2, m_send, m_recv,
):
    devices = n_bank * n_lane
    _, blocks, rows, lanes = a_ref.shape
    group = blocks * rows // devices
    groups = rows // group
    bank, lane = lax.axis_index("bank"), lax.axis_index("lane")
    me = bank * n_lane + lane

    fetches = [
        pltpu.make_async_copy(src, dst, in_sem.at[i])
        for i, (src, dst) in enumerate([
            (e_hbm, e_ref), (a_hbm, a_ref), (angle_hbm, angle_ref), (table_hbm, table_ref),
        ])
    ]
    for fetch in fetches:
        fetch.start()

    def others(act):
        half = n_lane // 2

        def around(step, first_bank):
            there = lax.rem(lane + half + step, n_lane)
            for turn in range(first_bank, n_bank):
                act(lax.rem(bank + turn, n_bank), there)
            return 0

        lax.fori_loop(0, half, lambda step, _: around(step, 0), 0)
        lax.fori_loop(half + 1, n_lane, lambda step, _: around(step, 0), 0)
        around(half, 1)

    barrier = pltpu.get_barrier_semaphore()

    def greet(to_bank, to_lane):
        pl.semaphore_signal(
            barrier, inc=1, device_id=(to_bank, to_lane), device_id_type=MESH
        )

    others(greet)
    fetches[0].wait()
    pl.semaphore_wait(barrier, devices - 1)

    def swap(src, dst, send_sem, recv_sem):
        def one(to_bank, to_lane):
            pltpu.make_async_remote_copy(
                src_ref=src.at[to_bank * n_lane + to_lane], dst_ref=dst.at[me],
                send_sem=send_sem, recv_sem=recv_sem,
                device_id=(to_bank, to_lane), device_id_type=MESH,
            ).start()

        others(one)

    def arrive(buffer, sem):
        most = buffer.at[pl.ds(0, devices - 1)]
        pltpu.make_async_copy(most, most, sem).wait()

    swap(e_ref, levels, e_send, e_recv)
    levels[me] = e_ref[me]
    for fetch in fetches[1:]:
        fetch.wait()

    table = table_ref[...]

    def block_step(b, _):
        first = b * groups
        level = e_ref[pl.ds(first, groups)].reshape(rows, lanes)
        c, s = cos_sin(level * angle_ref[0:1, :])
        re, im = a_ref[0, b], a_ref[1, b]
        turned = jnp.concatenate([re * c + im * s, im * c - re * s], axis=0)
        along = mix_lanes(turned, table)
        high, low = split(jnp.concatenate([along[:rows], along[rows:]], axis=1))
        mixed = dot(table[:128, :], jnp.concatenate([high, low], axis=0))
        held[b, 0] = mixed[:, :lanes]
        held[b, 1] = mixed[:, lanes:]
        return 0

    lax.fori_loop(0, blocks, block_step, 0)

    for chunk in range(chunks):
        def spread(g, _, chunk=chunk):
            start = pl.multiple_of(g * group + chunk * SUB, SUB)
            for part in range(2):
                mixed = mix([held[b, part, pl.ds(start, SUB), :] for b in range(blocks)])
                for b in range(blocks):
                    sent1[chunk, b * groups + g, part] = mixed[b]
            return 0

        lax.fori_loop(0, groups, spread, 0)
        swap(sent1.at[chunk], got1.at[chunk], send1.at[chunk], recv1.at[chunk])
        got1[chunk, me] = sent1[chunk, me]

    arrive(levels, e_recv)

    def phases(d, _):
        c, s = cos_sin(levels[d] * angle_ref[1:2, :])
        cosine[d] = c
        sine[d] = s
        return 0

    lax.fori_loop(0, devices, phases, 0)

    wide = TABLE // SUB
    lag = 2 if chunks > 1 else 1
    for chunk in range(chunks):
        arrive(got1.at[chunk], recv1.at[chunk])
        there = pl.ds(chunk * SUB, SUB)
        re = mix([got1[chunk, d, 0] for d in range(devices)])
        im = mix([got1[chunk, d, 1] for d in range(devices)])
        done = []
        for start in range(0, devices, wide):
            r, i = [], []
            for d in range(start, start + wide):
                c, s = cosine[d, there, :], sine[d, there, :]
                r.append(re[d] * c + im[d] * s)
                i.append(im[d] * c - re[d] * s)
            along = mix_lanes(jnp.concatenate(r + i, axis=0), table)
            pair = jnp.concatenate([along[:TABLE], along[TABLE:]], axis=1)
            high, low = split(pair)
            done.append(dot(table, high) + dot(table, low))
        done = mix(done)
        for d in range(devices):
            at = d % wide * SUB
            for part in range(2):
                tile = done[d // wide][at : at + SUB, part * lanes : (part + 1) * lanes]
                if chunk % lag:
                    before = sent2[chunk - 1, d, part]
                    sent2[chunk - 1, d, part] = before + tile
                    sent2[chunk, d, part] = before - tile
                else:
                    sent2[chunk, d, part] = tile
        if chunk % lag == lag - 1:
            for ready in range(chunk - lag + 1, chunk + 1):
                swap(sent2.at[ready], got2.at[ready], send2.at[ready], recv2.at[ready])
                got2[ready, me] = sent2[ready, me]

    scale = float(TABLE * TABLE) / (devices * blocks * rows * lanes)
    pieces = lag
    layers = chunks // pieces
    share = rows // n_bank // group

    def back(chunk, part):
        return mix([got2[chunk, d, part] for d in range(devices)])

    for chunk in range(chunks - pieces):
        arrive(got2.at[chunk], recv2.at[chunk])
        for part in range(2):
            mixed = back(chunk, part)
            for d in range(devices):
                got2[chunk, d, part] = mixed[d]

    copies = []
    for piece in range(pieces):
        last = chunks - pieces + piece
        arrive(got2.at[last], recv2.at[last])
        for part in range(2):
            mixed = back(last, part)
            for d in range(devices):
                tiles = [got2[t, d, part] for t in range(piece, last, pieces)]
                tiles = mix(tiles + [mixed[d]])
                b, g = divmod(d, groups)
                for t in range(layers):
                    value = tiles[t] * scale
                    at = g * group + (t * pieces + piece) * SUB
                    out_ref[part, b, at : at + SUB, :] = value
                    spot = (piece, g // share, b, pl.ds((g % share * layers + t) * SUB, SUB))
                    square = value * value
                    chance[spot] = chance[spot] + square if part else square
        for step in range(1, n_bank):
            other = lax.rem(bank + step, n_bank)
            copies.append(pltpu.make_async_remote_copy(
                src_ref=chance.at[piece, other], dst_ref=chances.at[piece, step - 1],
                send_sem=m_send.at[piece, step - 1], recv_sem=m_recv.at[piece, step - 1],
                device_id=(other, lane), device_id_type=MESH,
            ))
            copies[-1].start()
    for piece in range(pieces):
        for copy in copies[piece * (n_bank - 1) : (piece + 1) * (n_bank - 1)]:
            copy.wait_recv()
        total = chance[piece, bank]
        for step in range(1, n_bank):
            total = total + chances[piece, step - 1]
        total = total * (1.0 / n_bank)
        for g in range(share):
            for t in range(layers):
                at = g * group + (t * pieces + piece) * SUB
                of = (g * layers + t) * SUB
                marginal_ref[:, at : at + SUB, :] = total[:, of : of + SUB]

    for copy in copies:
        copy.wait_send()
    arrive(e_ref, e_send)
    for chunk in range(chunks):
        arrive(sent1.at[chunk], send1.at[chunk])
        arrive(sent2.at[chunk], send2.at[chunk])


def put_out(state_ref, marginal_ref, state_out, marginal_out, sem):
    copies = [
        pltpu.make_async_copy(state_ref, state_out, sem.at[0]),
        pltpu.make_async_copy(marginal_ref, marginal_out, sem.at[1]),
    ]
    for copy in copies:
        copy.start()
    for copy in copies:
        copy.wait()


def shards(n_bank, n_lane, amplitudes, energies, angles):
    devices = n_bank * n_lane
    _, blocks, rows, lanes = amplitudes.shape
    group = blocks * rows // devices
    chunks = group // SUB
    pieces = min(2, chunks)
    f32 = jnp.float32
    table = walsh_table()
    whole = pl.BlockSpec(memory_space=pltpu.VMEM)
    swapped = pltpu.VMEM((chunks, devices, 2, SUB, lanes), f32)
    real = pltpu.VMEM((devices, group, lanes), f32)
    strip = (blocks, rows // n_bank, lanes)
    part = (blocks, rows // n_bank // pieces, lanes)
    one, many = pltpu.SemaphoreType.DMA, pltpu.SemaphoreType.DMA((chunks,))
    state, marginal = pl.pallas_call(
        functools.partial(kernel, n_bank, n_lane, chunks),
        out_shape=(
            pltpu.VMEM(amplitudes.shape, f32),
            pltpu.VMEM(strip, f32),
        ),
        in_specs=[pl.BlockSpec(memory_space=pltpu.HBM)] * 4,
        out_specs=(whole, whole),
        scratch_shapes=[
            pltpu.VMEM(amplitudes.shape, f32),
            real,
            pltpu.VMEM(angles.shape, f32),
            pltpu.VMEM(table.shape, table.dtype),
            pltpu.VMEM((blocks, 2, rows, lanes), f32),
            swapped, swapped, swapped, swapped,
            real, real, real,
            pltpu.VMEM((pieces, n_bank, *part), f32),
            pltpu.VMEM((pieces, n_bank - 1, *part), f32),
            pltpu.SemaphoreType.DMA((4,)),
            one, one, many, many, many, many,
            pltpu.SemaphoreType.DMA((pieces, n_bank - 1)),
            pltpu.SemaphoreType.DMA((pieces, n_bank - 1)),
        ],
        compiler_params=pltpu.CompilerParams(
            collective_id=0, has_side_effects=True
        ),
        name="walsh",
    )(amplitudes, energies.reshape(devices, group, lanes), angles, table)
    return pl.pallas_call(
        put_out,
        out_shape=(
            jax.ShapeDtypeStruct(state.shape, f32),
            jax.ShapeDtypeStruct(marginal.shape, f32),
        ),
        in_specs=[whole] * 2,
        out_specs=(pl.BlockSpec(memory_space=pltpu.HBM),) * 2,
        scratch_shapes=[pltpu.SemaphoreType.DMA((2,))],
        compiler_params=pltpu.CompilerParams(vmem_limit_bytes=1024 * 1024),
        name="put_out",
    )(state, marginal)


def solution(mesh):
    sizes = mesh.shape
    return jax.shard_map(
        functools.partial(shards, sizes["bank"], sizes["lane"]),
        mesh=mesh,
        in_specs=(P(None, ("bank", "lane"), None, None), P(("bank", "lane"), None, None), P()),
        out_specs=(P(None, ("bank", "lane"), None, None), P("lane", "bank", None)),
        check_vma=False,
    )
```

profile of v0, /device:TPU:1, one launch (start us, length us, event | category | flops | bytes accessed | tf_op | source)
XLA Modules:
  0.0 71.6 jit_solution(15166180254858112888)
XLA Ops:
  0.6 70.0 %walsh.1 = (f32[2,8,128,128]{3,2,1,0:T(8,128)S(1)}, f32[8,32,128]{2,1,0:T(8,128)S(1)}) custom-call(f32[2,8,128,128]{3,2,1,0:T(8,128)} %a_hbm.1, f32[32,32,128]{2,1,0:T(8,128)} %bitcast.1, f32[2,128]{1,0:T(2,128)} %angle_hbm.1, bf16[256,256]{1,0:T(8,128)(2,1)} %constant.2.clone.table_hbm), custom_call_target="tpu_custom_call" | custom-call | tf_op jit(solution)/shard_map/walsh/pallas_call | solution.py:288
  70.6 1.0 %put_out.1 = (f32[2,8,128,128]{3,2,1,0:T(8,128)}, f32[8,32,128]{2,1,0:T(8,128)}) custom-call(f32[2,8,128,128]{3,2,1,0:T(8,128)S(1)} %get-tuple-element.4.state_ref, f32[8,32,128]{2,1,0:T(8,128)S(1)} %get-tuple-element.5.marginal_ref), custom_call_target="tpu_custom_call" | custom-call | tf_op jit(solution)/shard_map/put_out/pallas_call | solution.py:316
where the time goes:
time: 71.8 us; the launch traced here: 71.6 us
  Pallas kernels  71 us (99%)
    pallas_call x1, Pallas kernels, shards(): pl.pallas_call(functools.partial(kernel, n_bank, n_lane, chunks), out_sha...  70 us

commit v1 on v0

--- a/solution.py
+++ b/solution.py
@@ -83,17 +83,21 @@
         fetch.start()
 
     def others(act):
-        half = n_lane // 2
-
-        def around(step, first_bank):
-            there = lax.rem(lane + half + step, n_lane)
-            for turn in range(first_bank, n_bank):
+        low = lane < n_lane // 2
+
+        def around(step, _):
+            pair = step - lax.rem(step, 2)
+            there = jnp.where(low, n_lane - 2 - pair, pair) + lax.rem(step + lane, 2)
+            for turn in range(1, n_bank):
                 act(lax.rem(bank + turn, n_bank), there)
+
+            @pl.when(there != lane)
+            def _():
+                act(bank, there)
+
             return 0
 
-        lax.fori_loop(0, half, lambda step, _: around(step, 0), 0)
-        lax.fori_loop(half + 1, n_lane, lambda step, _: around(step, 0), 0)
-        around(half, 1)
+        lax.fori_loop(0, n_lane, around, 0)
 
     barrier = pltpu.get_barrier_semaphore()
 
@@ -165,8 +169,12 @@
 
     lax.fori_loop(0, devices, phases, 0)
 
+    def send_back(chunk):
+        swap(sent2.at[chunk], got2.at[chunk], send2.at[chunk], recv2.at[chunk])
+        got2[chunk, me] = sent2[chunk, me]
+
     wide = TABLE // SUB
-    lag = 2 if chunks > 1 else 1
+    half = max(chunks // 2, 1)
     for chunk in range(chunks):
         arrive(got1.at[chunk], recv1.at[chunk])
         there = pl.ds(chunk * SUB, SUB)
@@ -184,76 +192,90 @@
             high, low = split(pair)
             done.append(dot(table, high) + dot(table, low))
         done = mix(done)
+        first = chunk - chunk % half
+        last = chunk % half == half - 1
         for d in range(devices):
             at = d % wide * SUB
             for part in range(2):
                 tile = done[d // wide][at : at + SUB, part * lanes : (part + 1) * lanes]
-                if chunk % lag:
-                    before = sent2[chunk - 1, d, part]
-                    sent2[chunk - 1, d, part] = before + tile
-                    sent2[chunk, d, part] = before - tile
+                if last:
+                    tiles = mix([sent2[c, d, part] for c in range(first, chunk)] + [tile])
+                    for c in range(half):
+                        sent2[first + c, d, part] = tiles[c]
                 else:
                     sent2[chunk, d, part] = tile
-        if chunk % lag == lag - 1:
-            for ready in range(chunk - lag + 1, chunk + 1):
-                swap(sent2.at[ready], got2.at[ready], send2.at[ready], recv2.at[ready])
-                got2[ready, me] = sent2[ready, me]
+        if last:
+            send_back(first)
+
+    for chunk in range(1, half):
+        def halves(d, _, chunk=chunk):
+            for part in range(2):
+                u, v = sent2[chunk, d, part], sent2[chunk + half, d, part]
+                sent2[chunk, d, part] = u + v
+                sent2[chunk + half, d, part] = u - v
+            return 0
+
+        lax.fori_loop(0, devices, halves, 0)
 
     scale = float(TABLE * TABLE) / (devices * blocks * rows * lanes)
-    pieces = lag
-    layers = chunks // pieces
     share = rows // n_bank // group
+    steps = [(0, half)] if chunks > 1 else [(0,)]
+    steps += [(c,) for first in range(1, half) for c in (first, first + half)]
+    queue = [c for step in steps[1:] for c in step]
+    if queue:
+        send_back(queue.pop(0))
 
     def back(chunk, part):
         return mix([got2[chunk, d, part] for d in range(devices)])
 
-    for chunk in range(chunks - pieces):
-        arrive(got2.at[chunk], recv2.at[chunk])
+    copies = {}
+    for step in steps:
+        for chunk in step[:-1]:
+            arrive(got2.at[chunk], recv2.at[chunk])
+            for part in range(2):
+                mixed = back(chunk, part)
+                for d in range(devices):
+                    got2[chunk, d, part] = mixed[d]
+        arrive(got2.at[step[-1]], recv2.at[step[-1]])
         for part in range(2):
-            mixed = back(chunk, part)
+            mixed = back(step[-1], part)
             for d in range(devices):
-                got2[chunk, d, part] = mixed[d]
-
-    copies = []
-    for piece in range(pieces):
-        last = chunks - pieces + piece
-        arrive(got2.at[last], recv2.at[last])
-        for part in range(2):
-            mixed = back(last, part)
-            for d in range(devices):
-                tiles = [got2[t, d, part] for t in range(piece, last, pieces)]
-                tiles = mix(tiles + [mixed[d]])
+                tiles = mix([got2[c, d, part] for c in step[:-1]] + [mixed[d]])
                 b, g = divmod(d, groups)
-                for t in range(layers):
-                    value = tiles[t] * scale
-                    at = g * group + (t * pieces + piece) * SUB
+                for chunk, tile in zip(step, tiles):
+                    value = tile * scale
+                    at = g * group + chunk * SUB
                     out_ref[part, b, at : at + SUB, :] = value
-                    spot = (piece, g // share, b, pl.ds((g % share * layers + t) * SUB, SUB))
+                    spot = (chunk, g // share, b, pl.ds(g % share * SUB, SUB))
                     square = value * value
                     chance[spot] = chance[spot] + square if part else square
-        for step in range(1, n_bank):
-            other = lax.rem(bank + step, n_bank)
-            copies.append(pltpu.make_async_remote_copy(
-                src_ref=chance.at[piece, other], dst_ref=chances.at[piece, step - 1],
-                send_sem=m_send.at[piece, step - 1], recv_sem=m_recv.at[piece, step - 1],
-                device_id=(other, lane), device_id_type=MESH,
-            ))
-            copies[-1].start()
-    for piece in range(pieces):
-        for copy in copies[piece * (n_bank - 1) : (piece + 1) * (n_bank - 1)]:
-            copy.wait_recv()
-        total = chance[piece, bank]
-        for step in range(1, n_bank):
-            total = total + chances[piece, step - 1]
-        total = total * (1.0 / n_bank)
-        for g in range(share):
-            for t in range(layers):
-                at = g * group + (t * pieces + piece) * SUB
-                of = (g * layers + t) * SUB
-                marginal_ref[:, at : at + SUB, :] = total[:, of : of + SUB]
-
-    for copy in copies:
-        copy.wait_send()
+        for chunk in step:
+            copies[chunk] = []
+            for turn in range(1, n_bank):
+                other = lax.rem(bank + turn, n_bank)
+                copies[chunk].append(pltpu.make_async_remote_copy(
+                    src_ref=chance.at[chunk, other], dst_ref=chances.at[chunk, turn - 1],
+                    send_sem=m_send.at[chunk, turn - 1], recv_sem=m_recv.at[chunk, turn - 1],
+                    device_id=(other, lane), device_id_type=MESH,
+                ))
+                copies[chunk][-1].start()
+        if queue:
+            send_back(queue.pop(0))
+    for step in steps:
+        for chunk in step:
+            for copy in copies[chunk]:
+                copy.wait_recv()
+            total = chance[chunk, bank]
+            for turn in range(1, n_bank):
+                total = total + chances[chunk, turn - 1]
+            total = total * (1.0 / n_bank)
+            for g in range(share):
+                at = g * group + chunk * SUB
+                marginal_ref[:, at : at + SUB, :] = total[:, g * SUB : (g + 1) * SUB]
+
+    for chunk in range(chunks):
+        for copy in copies[chunk]:
+            copy.wait_send()
     arrive(e_ref, e_send)
     for chunk in range(chunks):
         arrive(sent1.at[chunk], send1.at[chunk])
@@ -276,14 +298,13 @@
     _, blocks, rows, lanes = amplitudes.shape
     group = blocks * rows // devices
     chunks = group // SUB
-    pieces = min(2, chunks)
     f32 = jnp.float32
     table = walsh_table()
     whole = pl.BlockSpec(memory_space=pltpu.VMEM)
     swapped = pltpu.VMEM((chunks, devices, 2, SUB, lanes), f32)
     real = pltpu.VMEM((devices, group, lanes), f32)
     strip = (blocks, rows // n_bank, lanes)
-    part = (blocks, rows // n_bank // pieces, lanes)
+    part = (blocks, rows // n_bank // chunks, lanes)
     one, many = pltpu.SemaphoreType.DMA, pltpu.SemaphoreType.DMA((chunks,))
     state, marginal = pl.pallas_call(
         functools.partial(kernel, n_bank, n_lane, chunks),
@@ -301,12 +322,12 @@
             pltpu.VMEM((blocks, 2, rows, lanes), f32),
             swapped, swapped, swapped, swapped,
             real, real, real,
-            pltpu.VMEM((pieces, n_bank, *part), f32),
-            pltpu.VMEM((pieces, n_bank - 1, *part), f32),
+            pltpu.VMEM((chunks, n_bank, *part), f32),
+            pltpu.VMEM((chunks, n_bank - 1, *part), f32),
             pltpu.SemaphoreType.DMA((4,)),
             one, one, many, many, many, many,
-            pltpu.SemaphoreType.DMA((pieces, n_bank - 1)),
-            pltpu.SemaphoreType.DMA((pieces, n_bank - 1)),
+            pltpu.SemaphoreType.DMA((chunks, n_bank - 1)),
+            pltpu.SemaphoreType.DMA((chunks, n_bank - 1)),
         ],
         compiler_params=pltpu.CompilerParams(
             collective_id=0, has_side_effects=True

time: 71.8 us -> 70.1 us (0.976)
  the two profiles are of different devices: /device:TPU:1 before, /device:TPU:9 now
where the time goes in v1:
time: 70.1 us; the launch traced here: 69.2 us
  Pallas kernels  68.6 us (98%)
    pallas_call x1, Pallas kernels, shards(): pl.pallas_call(functools.partial(kernel, n_bank, n_lane, chunks), out_sha...  67.5 us

profile of v1, /device:TPU:9, one launch (start us, length us, event | category | flops | bytes accessed | tf_op | source)
XLA Modules:
  0.0 69.2 jit_solution(8840694319537272724)
XLA Ops:
  0.6 67.5 %walsh.1 = (f32[2,8,128,128]{3,2,1,0:T(8,128)S(1)}, f32[8,32,128]{2,1,0:T(8,128)S(1)}) custom-call(f32[2,8,128,128]{3,2,1,0:T(8,128)} %a_hbm.1, f32[32,32,128]{2,1,0:T(8,128)} %bitcast.1, f32[2,128]{1,0:T(2,128)} %angle_hbm.1, bf16[256,256]{1,0:T(8,128)(2,1)} %constant.2.clone.table_hbm), custom_call_target="tpu_custom_call" | custom-call | tf_op jit(solution)/shard_map/walsh/pallas_call | solution.py:309
  68.2 1.0 %put_out.1 = (f32[2,8,128,128]{3,2,1,0:T(8,128)}, f32[8,32,128]{2,1,0:T(8,128)}) custom-call(f32[2,8,128,128]{3,2,1,0:T(8,128)S(1)} %get-tuple-element.4.state_ref, f32[8,32,128]{2,1,0:T(8,128)S(1)} %get-tuple-element.5.marginal_ref), custom_call_target="tpu_custom_call" | custom-call | tf_op jit(solution)/shard_map/put_out/pallas_call | solution.py:337

commit v2 on v1

--- a/solution.py
+++ b/solution.py
@@ -2,7 +2,6 @@
 
 import jax
 import jax.numpy as jnp
-import numpy as np
 from jax import lax
 from jax.experimental import pallas as pl
 from jax.experimental.pallas import tpu as pltpu
@@ -11,13 +10,17 @@
 MESH = pl.DeviceIdType.MESH
 TABLE = 256
 SUB = 8
+HALF = SUB // 2
+PLANES = 4
 
 
 def walsh_table():
-    rank = np.arange(TABLE)
-    both = rank[:, None] & rank[None, :]
-    parity = sum((both >> place) & 1 for place in range(8)) % 2
-    return jnp.asarray(np.where(parity == 1, -1.0, 1.0) / 16.0, jnp.bfloat16)
+    both = lax.broadcasted_iota(jnp.int32, (TABLE, TABLE), 0)
+    both = both & lax.broadcasted_iota(jnp.int32, (TABLE, TABLE), 1)
+    for place in (4, 2, 1):
+        both = both ^ (both >> place)
+    sign = 1 - 2 * (both & 1)
+    return (sign.astype(jnp.float32) * (1.0 / 16.0)).astype(jnp.bfloat16)
 
 
 def cos_sin(turn):
@@ -60,10 +63,11 @@
 
 def kernel(
     n_bank, n_lane, chunks,
-    a_hbm, e_hbm, angle_hbm, table_hbm,
+    a_hbm, e_hbm, angle_hbm,
     out_ref, marginal_ref,
     a_ref, e_ref, angle_ref, table_ref,
-    held, sent1, got1, sent2, got2, levels, cosine, sine, chance, chances,
+    held, sent1, got1, sent2, got2, levels, cosine, sine,
+    chance, chances, thin_chance, thin_chances,
     in_sem, e_send, e_recv, send1, recv1, send2, recv2, m_send, m_recv,
 ):
     devices = n_bank * n_lane
@@ -76,28 +80,35 @@
     fetches = [
         pltpu.make_async_copy(src, dst, in_sem.at[i])
         for i, (src, dst) in enumerate([
-            (e_hbm, e_ref), (a_hbm, a_ref), (angle_hbm, angle_ref), (table_hbm, table_ref),
+            (e_hbm, e_ref), (a_hbm, a_ref), (angle_hbm, angle_ref),
         ])
     ]
     for fetch in fetches:
         fetch.start()
 
-    def others(act):
-        low = lane < n_lane // 2
+    deep = n_lane // PLANES
+    lower = lane < n_lane // 2
+    plane = lane // deep
+    outer = (plane == 0) | (plane == PLANES - 1)
+
+    def to_plane(far, act):
+        first = jnp.where(lower, PLANES - 1 - far, far) * deep
 
         def around(step, _):
-            pair = step - lax.rem(step, 2)
-            there = jnp.where(low, n_lane - 2 - pair, pair) + lax.rem(step + lane, 2)
+            there = first + lax.rem(step + lane, deep)
             for turn in range(1, n_bank):
                 act(lax.rem(bank + turn, n_bank), there)
-
-            @pl.when(there != lane)
-            def _():
+            if far < PLANES // 2:
                 act(bank, there)
-
+            else:
+                pl.when(there != lane)(lambda: act(bank, there))
             return 0
 
-        lax.fori_loop(0, n_lane, around, 0)
+        lax.fori_loop(0, deep, around, 0)
+
+    def others(act):
+        for far in range(PLANES):
+            to_plane(far, act)
 
     barrier = pltpu.get_barrier_semaphore()
 
@@ -107,21 +118,22 @@
         )
 
     others(greet)
+    table_ref[...] = walsh_table()
     fetches[0].wait()
     pl.semaphore_wait(barrier, devices - 1)
 
-    def swap(src, dst, send_sem, recv_sem):
-        def one(to_bank, to_lane):
-            pltpu.make_async_remote_copy(
-                src_ref=src.at[to_bank * n_lane + to_lane], dst_ref=dst.at[me],
-                send_sem=send_sem, recv_sem=recv_sem,
-                device_id=(to_bank, to_lane), device_id_type=MESH,
-            ).start()
-
-        others(one)
-
-    def arrive(buffer, sem):
-        most = buffer.at[pl.ds(0, devices - 1)]
+    def give(src, dst, send_sem, recv_sem, to_bank, to_lane, spot=()):
+        pltpu.make_async_remote_copy(
+            src_ref=src.at[(to_bank * n_lane + to_lane, *spot)], dst_ref=dst.at[(me, *spot)],
+            send_sem=send_sem, recv_sem=recv_sem,
+            device_id=(to_bank, to_lane), device_id_type=MESH,
+        ).start()
+
+    def swap(*ends):
+        others(functools.partial(give, *ends))
+
+    def arrive(buffer, sem, spot=()):
+        most = buffer.at[(pl.ds(0, devices - 1), *spot)]
         pltpu.make_async_copy(most, most, sem).wait()
 
     swap(e_ref, levels, e_send, e_recv)
@@ -169,14 +181,35 @@
 
     lax.fori_loop(0, devices, phases, 0)
 
-    def send_back(chunk):
-        swap(sent2.at[chunk], got2.at[chunk], send2.at[chunk], recv2.at[chunk])
-        got2[chunk, me] = sent2[chunk, me]
-
     wide = TABLE // SUB
     half = max(chunks // 2, 1)
+    thin = chunks - 1 if half > 1 else chunks
+    messages = [(c, ()) for c in range(thin)]
+    messages += [(c, (h,)) for c in range(thin, chunks) for h in range(2)]
+
+    def give_back(at, far):
+        chunk, spot = messages[at]
+        ends = sent2.at[chunk], got2.at[chunk], send2.at[at], recv2.at[at]
+        to_plane(far, lambda b, l: give(*ends, b, l, spot))
+
+    def send_back(order):
+        for at, far in order:
+            give_back(at, far)
+        for at in sorted({at for at, _ in order}):
+            chunk, spot = messages[at]
+            got2[(chunk, me, *spot)] = sent2[(chunk, me, *spot)]
+
+    def far_first(*those):
+        return [(at, far) for at in those for far in range(PLANES)]
+
+    def take_back(at):
+        chunk, spot = messages[at]
+        arrive(got2.at[chunk], recv2.at[at], spot)
+
     for chunk in range(chunks):
         arrive(got1.at[chunk], recv1.at[chunk])
+        if chunk == chunks - 1 > 0:
+            pl.when(outer)(lambda: send_back(far_first(0)))
         there = pl.ds(chunk * SUB, SUB)
         re = mix([got1[chunk, d, 0] for d in range(devices)])
         im = mix([got1[chunk, d, 1] for d in range(devices)])
@@ -204,15 +237,26 @@
                         sent2[first + c, d, part] = tiles[c]
                 else:
                     sent2[chunk, d, part] = tile
-        if last:
-            send_back(first)
+        if last and first == chunk + 1 - chunks:
+            send_back(far_first(first))
+        elif last and first == 0:
+            pl.when(jnp.logical_not(outer))(lambda: send_back(far_first(0)))
+        elif last:
+            send_back(far_first(first))
 
     for chunk in range(1, half):
         def halves(d, _, chunk=chunk):
+            differ = []
             for part in range(2):
                 u, v = sent2[chunk, d, part], sent2[chunk + half, d, part]
                 sent2[chunk, d, part] = u + v
-                sent2[chunk + half, d, part] = u - v
+                differ.append(u - v)
+            for h in range(2):
+                tile = differ[h]
+                if chunk + half == thin:
+                    rows_h = slice(h * HALF, (h + 1) * HALF)
+                    tile = jnp.concatenate([part[rows_h] for part in differ], axis=0)
+                sent2[chunk + half, d, h] = tile
             return 0
 
         lax.fori_loop(0, devices, halves, 0)
@@ -221,22 +265,24 @@
     share = rows // n_bank // group
     steps = [(0, half)] if chunks > 1 else [(0,)]
     steps += [(c,) for first in range(1, half) for c in (first, first + half)]
-    queue = [c for step in steps[1:] for c in step]
-    if queue:
-        send_back(queue.pop(0))
+    steps[-1:] = [(at,) for at in range(thin, len(messages))] or steps[-1:]
+    if len(messages) > chunks:
+        send_back(far_first(*[at for (at,) in steps[1:-3]]))
+        x, y, z = [at for (at,) in steps[-3:]]
+        order = [(x, 0), (y, 0), (z, 0), (x, 1), (y, 1), (z, 1)]
+        send_back(order + [(at, far) for at in (x, y, z) for far in (2, 3)])
 
     def back(chunk, part):
         return mix([got2[chunk, d, part] for d in range(devices)])
 
-    copies = {}
-    for step in steps:
+    def whole(step):
         for chunk in step[:-1]:
-            arrive(got2.at[chunk], recv2.at[chunk])
+            take_back(chunk)
             for part in range(2):
                 mixed = back(chunk, part)
                 for d in range(devices):
                     got2[chunk, d, part] = mixed[d]
-        arrive(got2.at[step[-1]], recv2.at[step[-1]])
+        take_back(step[-1])
         for part in range(2):
             mixed = back(step[-1], part)
             for d in range(devices):
@@ -249,37 +295,73 @@
                     spot = (chunk, g // share, b, pl.ds(g % share * SUB, SUB))
                     square = value * value
                     chance[spot] = chance[spot] + square if part else square
-        for chunk in step:
-            copies[chunk] = []
+
+    def thinner(at):
+        take_back(at)
+        chunk, (h,) = messages[at]
+        mixed = back(chunk, h)
+        for d in range(devices):
+            b, g = divmod(d, groups)
+            value = mixed[d] * scale
+            row = g * group + chunk * SUB + h * HALF
+            for part in range(2):
+                out_ref[part, b, row : row + HALF, :] = value[part * HALF : (part + 1) * HALF]
+            square = value * value
+            low, high = b % few, b // few
+            spot = (h, g // share, low, pl.ds(g % share * SUB + high * HALF, HALF))
+            thin_chance[spot] = square[:HALF] + square[HALF:]
+
+    few = blocks // 2
+    copies = {}
+    for step in steps:
+        if step[0] < thin:
+            whole(step)
+        else:
+            thinner(step[0])
+        for at in step:
+            src, dst, place = chance, chances, at
+            if at >= thin:
+                src, dst, place = thin_chance, thin_chances, at - thin
+            copies[at] = []
             for turn in range(1, n_bank):
                 other = lax.rem(bank + turn, n_bank)
-                copies[chunk].append(pltpu.make_async_remote_copy(
-                    src_ref=chance.at[chunk, other], dst_ref=chances.at[chunk, turn - 1],
-                    send_sem=m_send.at[chunk, turn - 1], recv_sem=m_recv.at[chunk, turn - 1],
+                copies[at].append(pltpu.make_async_remote_copy(
+                    src_ref=src.at[place, other], dst_ref=dst.at[place, turn - 1],
+                    send_sem=m_send.at[at, turn - 1], recv_sem=m_recv.at[at, turn - 1],
                     device_id=(other, lane), device_id_type=MESH,
                 ))
-                copies[chunk][-1].start()
-        if queue:
-            send_back(queue.pop(0))
+                copies[at][-1].start()
     for step in steps:
-        for chunk in step:
-            for copy in copies[chunk]:
+        for at in step:
+            for copy in copies[at]:
                 copy.wait_recv()
-            total = chance[chunk, bank]
+            src, dst, place = chance, chances, at
+            if at >= thin:
+                src, dst, place = thin_chance, thin_chances, at - thin
+            total = src[place, bank]
             for turn in range(1, n_bank):
-                total = total + chances[chunk, turn - 1]
+                total = total + dst[place, turn - 1]
             total = total * (1.0 / n_bank)
             for g in range(share):
-                at = g * group + chunk * SUB
-                marginal_ref[:, at : at + SUB, :] = total[:, g * SUB : (g + 1) * SUB]
-
-    for chunk in range(chunks):
-        for copy in copies[chunk]:
+                row = g * group + messages[at][0] * SUB
+                if at < thin:
+                    marginal_ref[:, row : row + SUB, :] = total[:, g * SUB : (g + 1) * SUB]
+                else:
+                    row = row + place * HALF
+                    for high in range(2):
+                        from_row = g * SUB + high * HALF
+                        marginal_ref[high * few : (high + 1) * few, row : row + HALF, :] = (
+                            total[:, from_row : from_row + HALF]
+                        )
+
+    for at in range(len(messages)):
+        for copy in copies[at]:
             copy.wait_send()
     arrive(e_ref, e_send)
     for chunk in range(chunks):
         arrive(sent1.at[chunk], send1.at[chunk])
-        arrive(sent2.at[chunk], send2.at[chunk])
+    for at, (chunk, spot) in enumerate(messages):
+        arrive(sent2.at[chunk], send2.at[at], spot)
 
 
 def put_out(state_ref, marginal_ref, state_out, marginal_out, sem):
@@ -299,41 +381,44 @@
     group = blocks * rows // devices
     chunks = group // SUB
     f32 = jnp.float32
-    table = walsh_table()
     whole = pl.BlockSpec(memory_space=pltpu.VMEM)
     swapped = pltpu.VMEM((chunks, devices, 2, SUB, lanes), f32)
     real = pltpu.VMEM((devices, group, lanes), f32)
     strip = (blocks, rows // n_bank, lanes)
     part = (blocks, rows // n_bank // chunks, lanes)
+    thin = (blocks // 2, rows // n_bank // chunks, lanes)
     one, many = pltpu.SemaphoreType.DMA, pltpu.SemaphoreType.DMA((chunks,))
+    more = pltpu.SemaphoreType.DMA((chunks + 1,))
     state, marginal = pl.pallas_call(
         functools.partial(kernel, n_bank, n_lane, chunks),
         out_shape=(
             pltpu.VMEM(amplitudes.shape, f32),
             pltpu.VMEM(strip, f32),
         ),
-        in_specs=[pl.BlockSpec(memory_space=pltpu.HBM)] * 4,
+        in_specs=[pl.BlockSpec(memory_space=pltpu.HBM)] * 3,
         out_specs=(whole, whole),
         scratch_shapes=[
             pltpu.VMEM(amplitudes.shape, f32),
             real,
             pltpu.VMEM(angles.shape, f32),
-            pltpu.VMEM(table.shape, table.dtype),
+            pltpu.VMEM((TABLE, TABLE), jnp.bfloat16),
             pltpu.VMEM((blocks, 2, rows, lanes), f32),
             swapped, swapped, swapped, swapped,
             real, real, real,
             pltpu.VMEM((chunks, n_bank, *part), f32),
             pltpu.VMEM((chunks, n_bank - 1, *part), f32),
-            pltpu.SemaphoreType.DMA((4,)),
-            one, one, many, many, many, many,
-            pltpu.SemaphoreType.DMA((chunks, n_bank - 1)),
-            pltpu.SemaphoreType.DMA((chunks, n_bank - 1)),
+            pltpu.VMEM((2, n_bank, *thin), f32),
+            pltpu.VMEM((2, n_bank - 1, *thin), f32),
+            pltpu.SemaphoreType.DMA((3,)),
+            one, one, many, many, more, more,
+            pltpu.SemaphoreType.DMA((chunks + 1, n_bank - 1)),
+            pltpu.SemaphoreType.DMA((chunks + 1, n_bank - 1)),
         ],
         compiler_params=pltpu.CompilerParams(
             collective_id=0, has_side_effects=True
         ),
         name="walsh",
-    )(amplitudes, energies.reshape(devices, group, lanes), angles, table)
+    )(amplitudes, energies.reshape(devices, group, lanes), angles)
     return pl.pallas_call(
         put_out,
         out_shape=(

time: 70.1 us -> 68.9 us (0.983); the launches traced: 69.2 us -> 68.8 us
  no operation moved by 1% of the time
where the time goes in v2:
time: 68.9 us; the launch traced here: 68.8 us
  Pallas kernels  68.1 us (99%)
    pallas_call x1, Pallas kernels, shards(): pl.pallas_call(functools.partial(kernel, n_bank, n_lane, chunks), out_sha...  67.1 us

profile of v2, /device:TPU:9, one launch (start us, length us, event | category | flops | bytes accessed | tf_op | source)
XLA Modules:
  0.0 68.8 jit_solution(12460022316229790904)
XLA Ops:
  0.6 67.1 %walsh.1 = (f32[2,8,128,128]{3,2,1,0:T(8,128)S(1)}, f32[8,32,128]{2,1,0:T(8,128)S(1)}) custom-call(f32[2,8,128,128]{3,2,1,0:T(8,128)} %a_hbm.1, f32[32,32,128]{2,1,0:T(8,128)} %bitcast.1, f32[2,128]{1,0:T(2,128)} %angle_hbm.1), custom_call_target="tpu_custom_call" | custom-call | tf_op jit(solution)/shard_map/walsh/pallas_call | solution.py:392
  67.8 1.0 %put_out.1 = (f32[2,8,128,128]{3,2,1,0:T(8,128)}, f32[8,32,128]{2,1,0:T(8,128)}) custom-call(f32[2,8,128,128]{3,2,1,0:T(8,128)S(1)} %get-tuple-element.4.state_ref, f32[8,32,128]{2,1,0:T(8,128)S(1)} %get-tuple-element.5.marginal_ref), custom_call_target="tpu_custom_call" | custom-call | tf_op jit(solution)/shard_map/put_out/pallas_call | solution.py:422

commit v3 on v2

--- a/solution.py
+++ b/solution.py
@@ -68,7 +68,7 @@
     a_ref, e_ref, angle_ref, table_ref,
     held, sent1, got1, sent2, got2, levels, cosine, sine,
     chance, chances, thin_chance, thin_chances,
-    in_sem, e_send, e_recv, send1, recv1, send2, recv2, m_send, m_recv,
+    in_sem, e_send, e_recv, send1, recv1, send2, recv2, m_send, m_recv, known,
 ):
     devices = n_bank * n_lane
     _, blocks, rows, lanes = a_ref.shape
@@ -95,7 +95,7 @@
         first = jnp.where(lower, PLANES - 1 - far, far) * deep
 
         def around(step, _):
-            there = first + lax.rem(step + lane, deep)
+            there = first + lax.rem(step + lane + 1, deep)
             for turn in range(1, n_bank):
                 act(lax.rem(bank + turn, n_bank), there)
             if far < PLANES // 2:
@@ -117,10 +117,27 @@
             barrier, inc=1, device_id=(to_bank, to_lane), device_id_type=MESH
         )
 
-    others(greet)
+    next_lane = (plane + 1 - 2 * lax.rem(plane, 2)) * deep + lax.rem(lane, deep)
+    mirror_lane = (PLANES - 1 - plane) * deep + lax.rem(lane, deep)
+
+    def tell(step, to_lane):
+        pl.semaphore_signal(
+            known.at[step], inc=1, device_id=(bank, to_lane), device_id_type=MESH
+        )
+
+    @pl.when(outer)
+    def _():
+        greet(bank, next_lane)
+        to_plane(3, greet)
+
+    @pl.when(jnp.logical_not(outer))
+    def _():
+        to_plane(1, greet)
+        greet(bank, next_lane)
+        to_plane(2, greet)
+
     table_ref[...] = walsh_table()
     fetches[0].wait()
-    pl.semaphore_wait(barrier, devices - 1)
 
     def give(src, dst, send_sem, recv_sem, to_bank, to_lane, spot=()):
         pltpu.make_async_remote_copy(
@@ -136,7 +153,32 @@
         most = buffer.at[(pl.ds(0, devices - 1), *spot)]
         pltpu.make_async_copy(most, most, sem).wait()
 
-    swap(e_ref, levels, e_send, e_recv)
+    give_e = functools.partial(give, e_ref, levels, e_send, e_recv)
+
+    @pl.when(outer)
+    def _():
+        pl.semaphore_wait(barrier, n_bank * deep)
+        tell(0, next_lane)
+        to_plane(3, give_e)
+        pl.semaphore_wait(known.at[0], 1)
+        to_plane(1, give_e)
+        to_plane(2, give_e)
+        pl.semaphore_wait(known.at[2], 1)
+        to_plane(0, give_e)
+
+    @pl.when(jnp.logical_not(outer))
+    def _():
+        pl.semaphore_wait(barrier, 2 * n_bank * deep)
+        tell(0, next_lane)
+        to_plane(1, give_e)
+        to_plane(2, give_e)
+        pl.semaphore_wait(known.at[0], 1)
+        tell(1, mirror_lane)
+        to_plane(3, give_e)
+        pl.semaphore_wait(known.at[1], 1)
+        tell(2, next_lane)
+        to_plane(0, give_e)
+
     levels[me] = e_ref[me]
     for fetch in fetches[1:]:
         fetch.wait()
@@ -183,9 +225,10 @@
 
     wide = TABLE // SUB
     half = max(chunks // 2, 1)
-    thin = chunks - 1 if half > 1 else chunks
-    messages = [(c, ()) for c in range(thin)]
-    messages += [(c, (h,)) for c in range(thin, chunks) for h in range(2)]
+    thin = (half - 1, chunks - 1) if half > 1 else ()
+    fat = [c for c in range(chunks) if c not in thin]
+    messages = [(c, ()) for c in fat] + [(c, (h,)) for c in thin for h in range(2)]
+    few = blocks // 2
 
     def give_back(at, far):
         chunk, spot = messages[at]
@@ -238,61 +281,59 @@
                 else:
                     sent2[chunk, d, part] = tile
         if last and first == chunk + 1 - chunks:
-            send_back(far_first(first))
+            send_back(far_first(0))
         elif last and first == 0:
             pl.when(jnp.logical_not(outer))(lambda: send_back(far_first(0)))
         elif last:
-            send_back(far_first(first))
+            send_back(far_first(fat.index(first)))
 
     for chunk in range(1, half):
         def halves(d, _, chunk=chunk):
-            differ = []
-            for part in range(2):
-                u, v = sent2[chunk, d, part], sent2[chunk + half, d, part]
-                sent2[chunk, d, part] = u + v
-                differ.append(u - v)
-            for h in range(2):
-                tile = differ[h]
-                if chunk + half == thin:
-                    rows_h = slice(h * HALF, (h + 1) * HALF)
-                    tile = jnp.concatenate([part[rows_h] for part in differ], axis=0)
-                sent2[chunk + half, d, h] = tile
+            u, v = sent2[chunk, d], sent2[chunk + half, d]
+            for to, both in ((chunk, u + v), (chunk + half, u - v)):
+                if to in thin:
+                    both = [
+                        jnp.concatenate([part[h * HALF : (h + 1) * HALF] for part in both])
+                        for h in range(2)
+                    ]
+                for i in range(2):
+                    sent2[to, d, i] = both[i]
             return 0
 
         lax.fori_loop(0, devices, halves, 0)
 
     scale = float(TABLE * TABLE) / (devices * blocks * rows * lanes)
     share = rows // n_bank // group
-    steps = [(0, half)] if chunks > 1 else [(0,)]
-    steps += [(c,) for first in range(1, half) for c in (first, first + half)]
-    steps[-1:] = [(at,) for at in range(thin, len(messages))] or steps[-1:]
-    if len(messages) > chunks:
-        send_back(far_first(*[at for (at,) in steps[1:-3]]))
-        x, y, z = [at for (at,) in steps[-3:]]
-        order = [(x, 0), (y, 0), (z, 0), (x, 1), (y, 1), (z, 1)]
-        send_back(order + [(at, far) for at in (x, y, z) for far in (2, 3)])
+    slim = list(range(len(fat), len(messages)))
+    steps = [(0, fat.index(half))] if chunks > 1 else [(0,)]
+    for first in range(1, half - 1):
+        steps += [(fat.index(c),) for c in (first, first + half)]
+        send_back(far_first(*steps[-2], *steps[-1]))
+    steps += [(at,) for at in slim]
+    send_back([(at, far) for at in slim for far in (2, 3)] + [(at, far) for far in (0, 1) for at in slim])
 
     def back(chunk, part):
         return mix([got2[chunk, d, part] for d in range(devices)])
 
     def whole(step):
-        for chunk in step[:-1]:
-            take_back(chunk)
+        places = [messages[at][0] for at in step]
+        for at, chunk in zip(step[:-1], places):
+            take_back(at)
             for part in range(2):
                 mixed = back(chunk, part)
                 for d in range(devices):
                     got2[chunk, d, part] = mixed[d]
         take_back(step[-1])
         for part in range(2):
-            mixed = back(step[-1], part)
+            mixed = back(places[-1], part)
             for d in range(devices):
-                tiles = mix([got2[c, d, part] for c in step[:-1]] + [mixed[d]])
+                tiles = mix([got2[c, d, part] for c in places[:-1]] + [mixed[d]])
                 b, g = divmod(d, groups)
-                for chunk, tile in zip(step, tiles):
+                for at, chunk, tile in zip(step, places, tiles):
                     value = tile * scale
-                    at = g * group + chunk * SUB
-                    out_ref[part, b, at : at + SUB, :] = value
-                    spot = (chunk, g // share, b, pl.ds(g % share * SUB, SUB))
+                    row = g * group + chunk * SUB
+                    out_ref[part, b, row : row + SUB, :] = value
+                    spot = (at, g // share, b, pl.ds(g % share * SUB, SUB))
                     square = value * value
                     chance[spot] = chance[spot] + square if part else square
 
@@ -308,20 +349,19 @@
                 out_ref[part, b, row : row + HALF, :] = value[part * HALF : (part + 1) * HALF]
             square = value * value
             low, high = b % few, b // few
-            spot = (h, g // share, low, pl.ds(g % share * SUB + high * HALF, HALF))
+            spot = (at - len(fat), g // share, low, pl.ds(g % share * SUB + high * HALF, HALF))
             thin_chance[spot] = square[:HALF] + square[HALF:]
 
-    few = blocks // 2
     copies = {}
     for step in steps:
-        if step[0] < thin:
+        if step[0] < len(fat):
             whole(step)
         else:
             thinner(step[0])
         for at in step:
             src, dst, place = chance, chances, at
-            if at >= thin:
-                src, dst, place = thin_chance, thin_chances, at - thin
+            if at >= len(fat):
+                src, dst, place = thin_chance, thin_chances, at - len(fat)
             copies[at] = []
             for turn in range(1, n_bank):
                 other = lax.rem(bank + turn, n_bank)
@@ -336,23 +376,24 @@
             for copy in copies[at]:
                 copy.wait_recv()
             src, dst, place = chance, chances, at
-            if at >= thin:
-                src, dst, place = thin_chance, thin_chances, at - thin
+            if at >= len(fat):
+                src, dst, place = thin_chance, thin_chances, at - len(fat)
             total = src[place, bank]
             for turn in range(1, n_bank):
                 total = total + dst[place, turn - 1]
             total = total * (1.0 / n_bank)
+            chunk, spot = messages[at]
             for g in range(share):
-                row = g * group + messages[at][0] * SUB
-                if at < thin:
+                row = g * group + chunk * SUB
+                if not spot:
                     marginal_ref[:, row : row + SUB, :] = total[:, g * SUB : (g + 1) * SUB]
-                else:
-                    row = row + place * HALF
-                    for high in range(2):
-                        from_row = g * SUB + high * HALF
-                        marginal_ref[high * few : (high + 1) * few, row : row + HALF, :] = (
-                            total[:, from_row : from_row + HALF]
-                        )
+                    continue
+                row = row + spot[0] * HALF
+                for high in range(2):
+                    at_row = g * SUB + high * HALF
+                    marginal_ref[high * few : (high + 1) * few, row : row + HALF, :] = (
+                        total[:, at_row : at_row + HALF]
+                    )
 
     for at in range(len(messages)):
         for copy in copies[at]:
@@ -387,8 +428,11 @@
     strip = (blocks, rows // n_bank, lanes)
     part = (blocks, rows // n_bank // chunks, lanes)
     thin = (blocks // 2, rows // n_bank // chunks, lanes)
+    n_thin = 4 if chunks > 2 else 0
+    n_fat = chunks - n_thin // 2
+    n_messages = n_fat + n_thin
     one, many = pltpu.SemaphoreType.DMA, pltpu.SemaphoreType.DMA((chunks,))
-    more = pltpu.SemaphoreType.DMA((chunks + 1,))
+    more = pltpu.SemaphoreType.DMA((n_messages,))
     state, marginal = pl.pallas_call(
         functools.partial(kernel, n_bank, n_lane, chunks),
         out_shape=(
@@ -405,14 +449,15 @@
             pltpu.VMEM((blocks, 2, rows, lanes), f32),
             swapped, swapped, swapped, swapped,
             real, real, real,
-            pltpu.VMEM((chunks, n_bank, *part), f32),
-            pltpu.VMEM((chunks, n_bank - 1, *part), f32),
-            pltpu.VMEM((2, n_bank, *thin), f32),
-            pltpu.VMEM((2, n_bank - 1, *thin), f32),
+            pltpu.VMEM((n_fat, n_bank, *part), f32),
+            pltpu.VMEM((n_fat, n_bank - 1, *part), f32),
+            pltpu.VMEM((max(n_thin, 1), n_bank, *thin), f32),
+            pltpu.VMEM((max(n_thin, 1), n_bank - 1, *thin), f32),
             pltpu.SemaphoreType.DMA((3,)),
             one, one, many, many, more, more,
-            pltpu.SemaphoreType.DMA((chunks + 1, n_bank - 1)),
-            pltpu.SemaphoreType.DMA((chunks + 1, n_bank - 1)),
+            pltpu.SemaphoreType.DMA((n_messages, n_bank - 1)),
+            pltpu.SemaphoreType.DMA((n_messages, n_bank - 1)),
+            pltpu.SemaphoreType.REGULAR((3,)),
         ],
         compiler_params=pltpu.CompilerParams(
             collective_id=0, has_side_effects=True

time: 68.9 us -> 67.6 us (0.981)
  Pallas kernels: 68.1 us -> 66.8 us
    pallas_call x1, Pallas kernels: 67.1 us -> 65.8 us  [shards(): pl.pallas_call(functools.partial(kernel, n_bank, n_lane, chunks), out_sha...]
where the time goes in v3:
time: 67.6 us; the launch traced here: 67.4 us
  Pallas kernels  66.8 us (99%)
    pallas_call x1, Pallas kernels, shards(): pl.pallas_call(functools.partial(kernel, n_bank, n_lane, chunks), out_sha...  65.8 us

profile of v3, /device:TPU:9, one launch (start us, length us, event | category | flops | bytes accessed | tf_op | source)
XLA Modules:
  0.0 67.4 jit_solution(17002918160376548039)
XLA Ops:
  0.6 65.8 %walsh.1 = (f32[2,8,128,128]{3,2,1,0:T(8,128)S(1)}, f32[8,32,128]{2,1,0:T(8,128)S(1)}) custom-call(f32[2,8,128,128]{3,2,1,0:T(8,128)} %a_hbm.1, f32[32,32,128]{2,1,0:T(8,128)} %bitcast.1, f32[2,128]{1,0:T(2,128)} %angle_hbm.1), custom_call_target="tpu_custom_call" | custom-call | tf_op jit(solution)/shard_map/walsh/pallas_call | solution.py:436
  66.4 1.0 %put_out.1 = (f32[2,8,128,128]{3,2,1,0:T(8,128)}, f32[8,32,128]{2,1,0:T(8,128)}) custom-call(f32[2,8,128,128]{3,2,1,0:T(8,128)S(1)} %get-tuple-element.4.state_ref, f32[8,32,128]{2,1,0:T(8,128)S(1)} %get-tuple-element.5.marginal_ref), custom_call_target="tpu_custom_call" | custom-call | tf_op jit(solution)/shard_map/put_out/pallas_call | solution.py:467

commit v4 on v3

--- a/solution.py
+++ b/solution.py
@@ -68,7 +68,7 @@
     a_ref, e_ref, angle_ref, table_ref,
     held, sent1, got1, sent2, got2, levels, cosine, sine,
     chance, chances, thin_chance, thin_chances,
-    in_sem, e_send, e_recv, send1, recv1, send2, recv2, m_send, m_recv, known,
+    in_sem, sent, e_recv, recv1, recv2, m_recv, known,
 ):
     devices = n_bank * n_lane
     _, blocks, rows, lanes = a_ref.shape
@@ -106,6 +106,29 @@
 
         lax.fori_loop(0, deep, around, 0)
 
+    def to_mirror(corner, act):
+        first = (PLANES - 1 - plane) * deep
+        pair = n_bank // 2
+        opposite = lax.rem(bank // pair + 1, 2) * pair
+
+        def around(step, _):
+            there = first + lax.rem(step + lane, deep)
+            for turn in range(pair):
+                act(opposite + turn, there)
+            return 0
+
+        def beside(step, _):
+            there = first + lax.rem(step + lane, deep)
+            for turn in range(pair):
+                act(bank // pair * pair + lax.rem(bank + turn, pair), there)
+            return 0
+
+        if corner:
+            lax.fori_loop(1, deep, around, 0)
+        else:
+            lax.fori_loop(0, deep, beside, 0)
+            around(0, 0)
+
     def others(act):
         for far in range(PLANES):
             to_plane(far, act)
@@ -132,9 +155,9 @@
 
     @pl.when(jnp.logical_not(outer))
     def _():
-        to_plane(1, greet)
+        to_plane(2, greet)
+        to_mirror(False, greet)
         greet(bank, next_lane)
-        to_plane(2, greet)
 
     table_ref[...] = walsh_table()
     fetches[0].wait()
@@ -149,11 +172,13 @@
     def swap(*ends):
         others(functools.partial(give, *ends))
 
+    def wait_for(buffer, sem):
+        pltpu.make_async_copy(buffer, buffer, sem).wait()
+
     def arrive(buffer, sem, spot=()):
-        most = buffer.at[(pl.ds(0, devices - 1), *spot)]
-        pltpu.make_async_copy(most, most, sem).wait()
-
-    give_e = functools.partial(give, e_ref, levels, e_send, e_recv)
+        wait_for(buffer.at[(pl.ds(0, devices - 1), *spot)], sem)
+
+    give_e = functools.partial(give, e_ref, levels, sent.at[0], e_recv)
 
     @pl.when(outer)
     def _():
@@ -168,10 +193,13 @@
 
     @pl.when(jnp.logical_not(outer))
     def _():
-        pl.semaphore_wait(barrier, 2 * n_bank * deep)
+        pl.semaphore_wait(barrier, 2 * n_bank * deep - n_bank // 2 * (deep - 1))
+        tell(3, mirror_lane)
+        to_mirror(False, give_e)
+        to_plane(2, give_e)
+        pl.semaphore_wait(known.at[3], 1)
         tell(0, next_lane)
-        to_plane(1, give_e)
-        to_plane(2, give_e)
+        to_mirror(True, give_e)
         pl.semaphore_wait(known.at[0], 1)
         tell(1, mirror_lane)
         to_plane(3, give_e)
@@ -210,7 +238,7 @@
             return 0
 
         lax.fori_loop(0, groups, spread, 0)
-        swap(sent1.at[chunk], got1.at[chunk], send1.at[chunk], recv1.at[chunk])
+        swap(sent1.at[chunk], got1.at[chunk], sent.at[1], recv1.at[chunk])
         got1[chunk, me] = sent1[chunk, me]
 
     arrive(levels, e_recv)
@@ -232,7 +260,7 @@
 
     def give_back(at, far):
         chunk, spot = messages[at]
-        ends = sent2.at[chunk], got2.at[chunk], send2.at[at], recv2.at[at]
+        ends = sent2.at[chunk], got2.at[chunk], sent.at[2], recv2.at[at]
         to_plane(far, lambda b, l: give(*ends, b, l, spot))
 
     def send_back(order):
@@ -352,32 +380,28 @@
             spot = (at - len(fat), g // share, low, pl.ds(g % share * SUB + high * HALF, HALF))
             thin_chance[spot] = square[:HALF] + square[HALF:]
 
-    copies = {}
     for step in steps:
         if step[0] < len(fat):
             whole(step)
         else:
             thinner(step[0])
         for at in step:
+            src, dst, place, group_sem = chance, chances, at, 3
+            if at >= len(fat):
+                src, dst, place, group_sem = thin_chance, thin_chances, at - len(fat), 4
+            for turn in range(1, n_bank):
+                other = lax.rem(bank + turn, n_bank)
+                pltpu.make_async_remote_copy(
+                    src_ref=src.at[place, other], dst_ref=dst.at[place, turn - 1],
+                    send_sem=sent.at[group_sem], recv_sem=m_recv.at[at],
+                    device_id=(other, lane), device_id_type=MESH,
+                ).start()
+    for step in steps:
+        for at in step:
             src, dst, place = chance, chances, at
             if at >= len(fat):
                 src, dst, place = thin_chance, thin_chances, at - len(fat)
-            copies[at] = []
-            for turn in range(1, n_bank):
-                other = lax.rem(bank + turn, n_bank)
-                copies[at].append(pltpu.make_async_remote_copy(
-                    src_ref=src.at[place, other], dst_ref=dst.at[place, turn - 1],
-                    send_sem=m_send.at[at, turn - 1], recv_sem=m_recv.at[at, turn - 1],
-                    device_id=(other, lane), device_id_type=MESH,
-                ))
-                copies[at][-1].start()
-    for step in steps:
-        for at in step:
-            for copy in copies[at]:
-                copy.wait_recv()
-            src, dst, place = chance, chances, at
-            if at >= len(fat):
-                src, dst, place = thin_chance, thin_chances, at - len(fat)
+            wait_for(dst.at[place], m_recv.at[at])
             total = src[place, bank]
             for turn in range(1, n_bank):
                 total = total + dst[place, turn - 1]
@@ -395,14 +419,12 @@
                         total[:, at_row : at_row + HALF]
                     )
 
-    for at in range(len(messages)):
-        for copy in copies[at]:
-            copy.wait_send()
-    arrive(e_ref, e_send)
-    for chunk in range(chunks):
-        arrive(sent1.at[chunk], send1.at[chunk])
-    for at, (chunk, spot) in enumerate(messages):
-        arrive(sent2.at[chunk], send2.at[at], spot)
+    wait_for(chances, sent.at[3])
+    if slim:
+        wait_for(thin_chances, sent.at[4])
+    arrive(e_ref, sent.at[0])
+    wait_for(sent1.at[:, pl.ds(0, devices - 1)], sent.at[1])
+    wait_for(sent2.at[:, pl.ds(0, devices - 1)], sent.at[2])
 
 
 def put_out(state_ref, marginal_ref, state_out, marginal_out, sem):
@@ -431,7 +453,6 @@
     n_thin = 4 if chunks > 2 else 0
     n_fat = chunks - n_thin // 2
     n_messages = n_fat + n_thin
-    one, many = pltpu.SemaphoreType.DMA, pltpu.SemaphoreType.DMA((chunks,))
     more = pltpu.SemaphoreType.DMA((n_messages,))
     state, marginal = pl.pallas_call(
         functools.partial(kernel, n_bank, n_lane, chunks),
@@ -454,10 +475,11 @@
             pltpu.VMEM((max(n_thin, 1), n_bank, *thin), f32),
             pltpu.VMEM((max(n_thin, 1), n_bank - 1, *thin), f32),
             pltpu.SemaphoreType.DMA((3,)),
-            one, one, many, many, more, more,
-            pltpu.SemaphoreType.DMA((n_messages, n_bank - 1)),
-            pltpu.SemaphoreType.DMA((n_messages, n_bank - 1)),
-            pltpu.SemaphoreType.REGULAR((3,)),
+            pltpu.SemaphoreType.DMA((5,)),
+            pltpu.SemaphoreType.DMA,
+            pltpu.SemaphoreType.DMA((chunks,)),
+            more, more,
+            pltpu.SemaphoreType.REGULAR((4,)),
         ],
         compiler_params=pltpu.CompilerParams(
             collective_id=0, has_side_effects=True

time: 67.6 us -> 67 us (level)
  no operation moved by 1% of the time
where the time goes in v4:
time: 67 us; the launch traced here: 66.9 us
  Pallas kernels  66.2 us (99%)
    pallas_call x1, Pallas kernels, shards(): pl.pallas_call(functools.partial(kernel, n_bank, n_lane, chunks), out_sha...  65.2 us

profile of v4, /device:TPU:9, one launch (start us, length us, event | category | flops | bytes accessed | tf_op | source)
XLA Modules:
  0.0 66.9 jit_solution(3897171205290031187)
XLA Ops:
  0.6 65.2 %walsh.1 = (f32[2,8,128,128]{3,2,1,0:T(8,128)S(1)}, f32[8,32,128]{2,1,0:T(8,128)S(1)}) custom-call(f32[2,8,128,128]{3,2,1,0:T(8,128)} %a_hbm.1, f32[32,32,128]{2,1,0:T(8,128)} %bitcast.1, f32[2,128]{1,0:T(2,128)} %angle_hbm.1), custom_call_target="tpu_custom_call" | custom-call | tf_op jit(solution)/shard_map/walsh/pallas_call | solution.py:457
  65.9 1.0 %put_out.1 = (f32[2,8,128,128]{3,2,1,0:T(8,128)}, f32[8,32,128]{2,1,0:T(8,128)}) custom-call(f32[2,8,128,128]{3,2,1,0:T(8,128)S(1)} %get-tuple-element.4.state_ref, f32[8,32,128]{2,1,0:T(8,128)S(1)} %get-tuple-element.5.marginal_ref), custom_call_target="tpu_custom_call" | custom-call | tf_op jit(solution)/shard_map/put_out/pallas_call | solution.py:489

commit v5 on v4

--- a/solution.py
+++ b/solution.py
@@ -91,11 +91,11 @@
     plane = lane // deep
     outer = (plane == 0) | (plane == PLANES - 1)
 
-    def to_plane(far, act):
-        first = jnp.where(lower, PLANES - 1 - far, far) * deep
+    def to_plane(far, act, start=0, count=deep):
+        first = jnp.where(lower, PLANES - 1 - far, far) * deep + start
 
         def around(step, _):
-            there = first + lax.rem(step + lane + 1, deep)
+            there = first + lax.rem(step + lane + 1, count)
             for turn in range(1, n_bank):
                 act(lax.rem(bank + turn, n_bank), there)
             if far < PLANES // 2:
@@ -104,7 +104,7 @@
                 pl.when(there != lane)(lambda: act(bank, there))
             return 0
 
-        lax.fori_loop(0, deep, around, 0)
+        lax.fori_loop(0, count, around, 0)
 
     def to_mirror(corner, act):
         first = (PLANES - 1 - plane) * deep
@@ -258,15 +258,15 @@
     messages = [(c, ()) for c in fat] + [(c, (h,)) for c in thin for h in range(2)]
     few = blocks // 2
 
-    def give_back(at, far):
+    def give_back(at, far, *some):
         chunk, spot = messages[at]
         ends = sent2.at[chunk], got2.at[chunk], sent.at[2], recv2.at[at]
-        to_plane(far, lambda b, l: give(*ends, b, l, spot))
+        to_plane(far, lambda b, l: give(*ends, b, l, spot), *some)
 
     def send_back(order):
-        for at, far in order:
-            give_back(at, far)
-        for at in sorted({at for at, _ in order}):
+        for at, far, *some in order:
+            give_back(at, far, *some)
+        for at in sorted({at for at, *_ in order}):
             chunk, spot = messages[at]
             got2[(chunk, me, *spot)] = sent2[(chunk, me, *spot)]
 
@@ -338,7 +338,11 @@
         steps += [(fat.index(c),) for c in (first, first + half)]
         send_back(far_first(*steps[-2], *steps[-1]))
     steps += [(at,) for at in slim]
-    send_back([(at, far) for at in slim for far in (2, 3)] + [(at, far) for far in (0, 1) for at in slim])
+    rows_of = [(far, start, deep // 2) for far in (0, 1) for start in (0, deep // 2)]
+    order = [(0, 0), (1, 0), (2, 0), (3, 0), (0, 1), (1, 1), (0, 2), (0, 3), (2, 1), (1, 2), (1, 3), (3, 1), (2, 2), (2, 3), (3, 2), (3, 3)]
+    send_back([(at, far) for at in slim for far in (2, 3)])
+    if slim:
+        send_back([(slim[i], *rows_of[j]) for i, j in order])
 
     def back(chunk, part):
         return mix([got2[chunk, d, part] for d in range(devices)])

time: 67 us -> 66.9 us (level)
  no operation moved by 1% of the time
where the time goes in v5:
time: 66.9 us; the launch traced here: 66.6 us
  Pallas kernels  66 us (99%)
    pallas_call x1, Pallas kernels, shards(): pl.pallas_call(functools.partial(kernel, n_bank, n_lane, chunks), out_sha...  65 us

profile of v5, /device:TPU:9, one launch (start us, length us, event | category | flops | bytes accessed | tf_op | source)
XLA Modules:
  0.0 66.6 jit_solution(10189657770195452981)
XLA Ops:
  0.6 65.0 %walsh.1 = (f32[2,8,128,128]{3,2,1,0:T(8,128)S(1)}, f32[8,32,128]{2,1,0:T(8,128)S(1)}) custom-call(f32[2,8,128,128]{3,2,1,0:T(8,128)} %a_hbm.1, f32[32,32,128]{2,1,0:T(8,128)} %bitcast.1, f32[2,128]{1,0:T(2,128)} %angle_hbm.1), custom_call_target="tpu_custom_call" | custom-call | tf_op jit(solution)/shard_map/walsh/pallas_call | solution.py:461
  65.6 1.0 %put_out.1 = (f32[2,8,128,128]{3,2,1,0:T(8,128)}, f32[8,32,128]{2,1,0:T(8,128)}) custom-call(f32[2,8,128,128]{3,2,1,0:T(8,128)S(1)} %get-tuple-element.4.state_ref, f32[8,32,128]{2,1,0:T(8,128)S(1)} %get-tuple-element.5.marginal_ref), custom_call_target="tpu_custom_call" | custom-call | tf_op jit(solution)/shard_map/put_out/pallas_call | solution.py:493

commit v6 on v5

--- a/solution.py
+++ b/solution.py
@@ -83,9 +83,6 @@
             (e_hbm, e_ref), (a_hbm, a_ref), (angle_hbm, angle_ref),
         ])
     ]
-    for fetch in fetches:
-        fetch.start()
-
     deep = n_lane // PLANES
     lower = lane < n_lane // 2
     plane = lane // deep
@@ -155,10 +152,12 @@
 
     @pl.when(jnp.logical_not(outer))
     def _():
-        to_plane(2, greet)
         to_mirror(False, greet)
         greet(bank, next_lane)
-
+        to_plane(2, greet)
+
+    for fetch in fetches:
+        fetch.start()
     table_ref[...] = walsh_table()
     fetches[0].wait()
 
@@ -397,15 +396,17 @@
                 other = lax.rem(bank + turn, n_bank)
                 pltpu.make_async_remote_copy(
                     src_ref=src.at[place, other], dst_ref=dst.at[place, turn - 1],
-                    send_sem=sent.at[group_sem], recv_sem=m_recv.at[at],
+                    send_sem=sent.at[group_sem], recv_sem=m_recv.at[group_sem - 3],
                     device_id=(other, lane), device_id_type=MESH,
                 ).start()
+    wait_for(chances, m_recv.at[0])
+    if slim:
+        wait_for(thin_chances, m_recv.at[1])
     for step in steps:
         for at in step:
             src, dst, place = chance, chances, at
             if at >= len(fat):
                 src, dst, place = thin_chance, thin_chances, at - len(fat)
-            wait_for(dst.at[place], m_recv.at[at])
             total = src[place, bank]
             for turn in range(1, n_bank):
                 total = total + dst[place, turn - 1]
@@ -482,7 +483,8 @@
             pltpu.SemaphoreType.DMA((5,)),
             pltpu.SemaphoreType.DMA,
             pltpu.SemaphoreType.DMA((chunks,)),
-            more, more,
+            more,
+            pltpu.SemaphoreType.DMA((2,)),
             pltpu.SemaphoreType.REGULAR((4,)),
         ],
         compiler_params=pltpu.CompilerParams(

time: 66.9 us -> 66.9 us (level)
  no operation moved by 1% of the time
where the time goes in v6:
time: 66.9 us; the launch traced here: 66.7 us
  Pallas kernels  66.1 us (99%)
    pallas_call x1, Pallas kernels, shards(): pl.pallas_call(functools.partial(kernel, n_bank, n_lane, chunks), out_sha...  65 us

profile of v6, /device:TPU:9, one launch (start us, length us, event | category | flops | bytes accessed | tf_op | source)
XLA Modules:
  0.0 66.7 jit_solution(14948203282672142691)
XLA Ops:
  0.6 65.0 %walsh.1 = (f32[2,8,128,128]{3,2,1,0:T(8,128)S(1)}, f32[8,32,128]{2,1,0:T(8,128)S(1)}) custom-call(f32[2,8,128,128]{3,2,1,0:T(8,128)} %a_hbm.1, f32[32,32,128]{2,1,0:T(8,128)} %bitcast.1, f32[2,128]{1,0:T(2,128)} %angle_hbm.1), custom_call_target="tpu_custom_call" | custom-call | tf_op jit(solution)/shard_map/walsh/pallas_call | solution.py:462
  65.7 1.0 %put_out.1 = (f32[2,8,128,128]{3,2,1,0:T(8,128)}, f32[8,32,128]{2,1,0:T(8,128)}) custom-call(f32[2,8,128,128]{3,2,1,0:T(8,128)S(1)} %get-tuple-element.4.state_ref, f32[8,32,128]{2,1,0:T(8,128)S(1)} %get-tuple-element.5.marginal_ref), custom_call_target="tpu_custom_call" | custom-call | tf_op jit(solution)/shard_map/put_out/pallas_call | solution.py:495

commit v7 on v6

--- a/solution.py
+++ b/solution.py
@@ -187,8 +187,6 @@
         pl.semaphore_wait(known.at[0], 1)
         to_plane(1, give_e)
         to_plane(2, give_e)
-        pl.semaphore_wait(known.at[2], 1)
-        to_plane(0, give_e)
 
     @pl.when(jnp.logical_not(outer))
     def _():
@@ -202,9 +200,6 @@
         pl.semaphore_wait(known.at[0], 1)
         tell(1, mirror_lane)
         to_plane(3, give_e)
-        pl.semaphore_wait(known.at[1], 1)
-        tell(2, next_lane)
-        to_plane(0, give_e)
 
     levels[me] = e_ref[me]
     for fetch in fetches[1:]:
@@ -226,6 +221,17 @@
         return 0
 
     lax.fori_loop(0, blocks, block_step, 0)
+
+    @pl.when(outer)
+    def _():
+        pl.semaphore_wait(known.at[2], 1)
+        to_plane(0, give_e)
+
+    @pl.when(jnp.logical_not(outer))
+    def _():
+        pl.semaphore_wait(known.at[1], 1)
+        tell(2, next_lane)
+        to_plane(0, give_e)
 
     for chunk in range(chunks):
         def spread(g, _, chunk=chunk):

time: 66.9 us -> 66.9 us (level)
  no operation moved by 1% of the time
where the time goes in v7:
time: 66.9 us; the launch traced here: 66.7 us
  Pallas kernels  66 us (99%)
    pallas_call x1, Pallas kernels, shards(): pl.pallas_call(functools.partial(kernel, n_bank, n_lane, chunks), out_sha...  65 us

profile of v7, /device:TPU:9, one launch (start us, length us, event | category | flops | bytes accessed | tf_op | source)
XLA Modules:
  0.0 66.7 jit_solution(18306499130657687766)
XLA Ops:
  0.6 65.0 %walsh.1 = (f32[2,8,128,128]{3,2,1,0:T(8,128)S(1)}, f32[8,32,128]{2,1,0:T(8,128)S(1)}) custom-call(f32[2,8,128,128]{3,2,1,0:T(8,128)} %a_hbm.1, f32[32,32,128]{2,1,0:T(8,128)} %bitcast.1, f32[2,128]{1,0:T(2,128)} %angle_hbm.1), custom_call_target="tpu_custom_call" | custom-call | tf_op jit(solution)/shard_map/walsh/pallas_call | solution.py:468
  65.7 1.0 %put_out.1 = (f32[2,8,128,128]{3,2,1,0:T(8,128)}, f32[8,32,128]{2,1,0:T(8,128)}) custom-call(f32[2,8,128,128]{3,2,1,0:T(8,128)S(1)} %get-tuple-element.4.state_ref, f32[8,32,128]{2,1,0:T(8,128)S(1)} %get-tuple-element.5.marginal_ref), custom_call_target="tpu_custom_call" | custom-call | tf_op jit(solution)/shard_map/put_out/pallas_call | solution.py:501
